TPU v7x, 32 devices: a whole 2x2x4 slice. The times are simulated.
32 devices in a mesh: dp: 2 (over x), tp: 4 (over z), ep: 4 (over y, core).
Axes of the slice: x: 2, y: 2, z: 4, core: 2. Of those that a mesh axis runs over, the one named last changes fastest.
Arguments:
- hidden_in: bfloat16 [8192, 2048], P(('dp', 'ep')), parts along dimension 0
- topk_idx: int32 [8192, 4], P(('dp', 'ep')), parts along dimension 0
- norm_gain: bfloat16 [2048], replicated
- router_w: bfloat16 [2048, 60], replicated
- shared_sig_w: bfloat16 [2048, 1], replicated
- exp_gate: bfloat16 [60, 2048, 1408], P('ep', None, 'tp')
- exp_up: bfloat16 [60, 2048, 1408], P('ep', None, 'tp')
- exp_down: bfloat16 [60, 1408, 2048], P('ep', 'tp')
- sh_gate: bfloat16 [2048, 5632], P(None, ('tp', 'ep'))
- sh_up: bfloat16 [2048, 5632], P(None, ('tp', 'ep'))
- sh_down: bfloat16 [5632, 2048], P(('tp', 'ep'))
Outputs:
- output: bfloat16 [8192, 2048], P(('dp', 'ep')), parts along dimension 0
There are 2 independent parts. A program takes and returns all parts, laid end to end along the dimension named above; an argument that names none is the same for every part.
All inputs are finite; a program needn't handle non-finite values.
Results may differ from a plain program's by a relative error of at most 0.0110312.
Values are sent between devices in bfloat16 or wider.
A program may use at most 1 GiB of HBM per device.

v0:
```python
import functools
import math

import jax
import jax.numpy as jnp
from jax import lax
from jax.experimental import pallas as pl
from jax.experimental.pallas import tpu as pltpu
from jax.sharding import PartitionSpec as P

RMS_EPS = 1e-6
LANES = 128
TILE = 256
PITCH = TILE + 1
GROUP = 8
TOK_MASK = 8191
MESH = pl.DeviceIdType.MESH
SPREAD_CHUNKS = 16
COMBINE_CHUNKS = 64
COMBINE_LAG = 3


def dot_t(a, b):
    return lax.dot_general(a, b, (((1,), (1,)), ((), ())), preferred_element_type=jnp.float32)


def routing(idx_ref, first, ranks, n_tok, n_local, n_row, pos_v, list_v, in_row, totals):
    n = idx_ref.shape[0]
    i32, bf16, f32 = jnp.int32, jnp.bfloat16, jnp.float32
    sub = lax.broadcasted_iota(i32, (LANES, LANES), 0)
    lane = lax.broadcasted_iota(i32, (LANES, LANES), 1)
    below = jnp.where(sub < lane, 1.0, 0.0).astype(bf16)
    above = jnp.where(lane < sub, 1.0, 0.0).astype(bf16)
    ones = jnp.ones((LANES, LANES), bf16)

    def mask(e):
        return jnp.where(idx_ref[...] == first + e, 1.0, 0.0)

    both = jnp.concatenate([below, ones], axis=1)
    for e in range(n_local):
        got = jnp.dot(mask(e).astype(bf16), both, preferred_element_type=f32)
        in_row[e * n:(e + 1) * n, :] = got[:, :LANES]
        totals[e * n:(e + 1) * n, :] = got[:, LANES:]
    pos = jnp.zeros((n, LANES), f32)
    start = jnp.zeros((1, LANES), i32)
    for e in range(n_local):
        total = totals[e * n:(e + 1) * n, :]
        before = jnp.dot(above, total.astype(bf16), preferred_element_type=f32)
        count = (before[n - 1:n] + total[n - 1:n]).astype(i32)
        tiles = (count + TILE - 1) // TILE
        list_v[n_row + e:n_row + e + 1, :] = tiles
        pos += mask(e) * (in_row[e * n:(e + 1) * n, :] + before + (start * TILE).astype(f32) + 1.0)
        start += tiles
    pos_v[...] = pos.astype(i32) - 1

    rows = lax.broadcasted_iota(i32, (n_row, LANES), 0)
    step = 8
    nb = n_tok // ranks // LANES
    n_top = n * LANES // n_tok
    base = n_tok // LANES
    lane_val = lax.broadcasted_iota(i32, (LANES, LANES), 1).astype(f32)

    def add(g, acc):
        lhs, rhs = [], []
        for u in range(step):
            r = g * step + u
            p = pos_v[pl.ds(r, 1), :]
            tok_row = r // (nb * n_top) * nb + r % nb
            code = (r // nb % n_top * ((TOK_MASK + 1) // LANES) + tok_row - base).astype(f32)
            lhs.append(jnp.where(rows == p // LANES, 1.0, 0.0).astype(bf16))
            hit = sub == jnp.where(p < 0, LANES, p % LANES)
            rhs.append(jnp.concatenate([jnp.where(hit, code, 0.0), jnp.where(hit, lane_val, 0.0)], axis=0).astype(bf16))
        return acc + dot_t(jnp.concatenate(lhs, axis=1), jnp.concatenate(rhs, axis=1))
    acc = lax.fori_loop(0, n // step, add, jnp.zeros((n_row, 2 * LANES), f32))
    list_v[0:n_row, :] = (acc[:, :LANES] * LANES + acc[:, LANES:]).astype(i32) + n_tok


def moe_kernel(idx_ref, wt_hbm, h_hbm, sum_hbm, eg, eu, ed, out_hbm,
               hv, acc, wg, wu, wd, x4, xb, act, y4, pos_v, list_v, list_ref, tile_exp, wt_ref, h_sem, s_sem, w_sem, o_sem, l_sem, t_sem):
    n_tok, chunks, _ = h_hbm.shape
    n_local, width, _ = ed.shape
    n_row = list_v.shape[0] - 16
    span = TILE // LANES
    last = n_row // span - 1

    def weight_copies(e, slot):
        return [pltpu.make_async_copy(s.at[e], d.at[slot], w_sem.at[slot, i])
                for i, (s, d) in enumerate(((eg, wg), (eu, wu), (ed, wd)))]

    h_copy = pltpu.make_async_copy(h_hbm, hv.at[pl.ds(0, n_tok)], h_sem)
    s_copy = pltpu.make_async_copy(sum_hbm, acc.at[pl.ds(0, n_tok)], s_sem)
    t_copy = pltpu.make_async_copy(wt_hbm, wt_ref, t_sem)
    h_copy.start()
    t_copy.start()
    s_copy.start()
    routing(idx_ref, lax.axis_index("ep") * n_local, lax.axis_size("ep"), n_tok, n_local, n_row, pos_v, list_v, x4, y4)
    l_copy = pltpu.make_async_copy(list_v, list_ref, l_sem)
    l_copy.start()
    l_copy.wait()

    def exp_tiles(e):
        return list_ref[n_row + e, 0]

    def fill(e, t):
        def put(j, _):
            tile_exp[t + j] = e
            return 0
        count = exp_tiles(e)
        lax.fori_loop(0, count, put, 0)
        return t + count
    n_tile = lax.fori_loop(0, n_local, fill, 0)

    @pl.when(n_tile > 0)
    def _():
        for c in weight_copies(tile_exp[0], 0):
            c.start()
    h_copy.wait()
    t_copy.wait()

    def gather(base, g):
        for u in range(GROUP):
            i = g * GROUP + u
            tok = list_ref[base * span + i // LANES, i % LANES] & TOK_MASK
            x4[pl.ds(i, chunks, stride=PITCH), :] = hv[tok].astype(jnp.float32)

    def pack(k):
        xb[:, k * LANES:(k + 1) * LANES] = x4[k * PITCH:k * PITCH + TILE, :].astype(jnp.bfloat16)

    def scatter(base, g):
        sums = []
        for u in range(GROUP):
            i = g * GROUP + u
            entry = list_ref[base * span + i // LANES, i % LANES]
            tok = entry & TOK_MASK
            sums.append((tok, acc[tok] + y4[pl.ds(i, chunks, stride=PITCH), :] * wt_ref[entry]))
        for tok, v in sums:
            acc[tok] = v

    def loop(fn, base):
        for g in range(TILE // GROUP):
            fn(base, g)

    loop(gather, 0)
    for k in range(chunks):
        pack(k)
    def tile(t, slot):
        e = tile_exp[t]
        fresh = (t == 0) | (e != tile_exp[jnp.maximum(t - 1, 0)])
        slot = jnp.where(fresh, 1 - slot, slot)

        @pl.when(fresh)
        def _():
            for c in weight_copies(e, slot):
                c.wait()
            after = t + exp_tiles(e)

            @pl.when(after < n_tile)
            def _():
                for c in weight_copies(tile_exp[after], 1 - slot):
                    c.start()

        @pl.when(t == 1)
        def _():
            s_copy.wait()

        prev = jnp.where(t == 0, last, t - 1)
        n_group = TILE // GROUP
        gate = dot_t(xb[...], wg[slot])
        up = dot_t(xb[...], wu[slot])
        for g in range(n_group):
            scatter(prev, g)
        act[...] = (jax.nn.silu(gate) * up).astype(jnp.bfloat16)
        for g in range(n_group):
            gather(t + 1, g)
        for k in range(0, chunks, 2):
            d = jnp.dot(act[...], wd[slot, :, k * LANES:(k + 2) * LANES], preferred_element_type=jnp.float32)
            y4[k * PITCH:k * PITCH + TILE, :] = d[:, :LANES]
            y4[(k + 1) * PITCH:(k + 1) * PITCH + TILE, :] = d[:, LANES:]
        for k in range(chunks):
            pack(k)
        return slot

    lax.fori_loop(0, n_tile, tile, 1)

    @pl.when(n_tile <= 1)
    def _():
        s_copy.wait()
    loop(scatter, jnp.where(n_tile == 0, last, n_tile - 1))

    blk = 256

    def flush(i, _):
        def conv(j, _):
            r = i * blk + j * 16
            hv[pl.ds(r, 16)] = acc[pl.ds(r, 16)].astype(jnp.bfloat16)
            return 0
        lax.fori_loop(0, blk // 16, conv, 0)
        pltpu.make_async_copy(hv.at[pl.ds(i * blk, blk)], out_hbm.at[pl.ds(i * blk, blk)], o_sem).start()
        return 0
    lax.fori_loop(0, n_tok // blk, flush, 0)
    pltpu.make_async_copy(hv.at[pl.ds(0, n_tok)], out_hbm, o_sem).wait()


def moe(idx, wt, h3, sums, eg, eu, ed):
    n_tok, chunks, _ = h3.shape
    hidden = chunks * LANES
    width = ed.shape[1]
    hbm = pl.BlockSpec(memory_space=pl.ANY)
    max_tiles = -(-(idx.size + eg.shape[0] * (TILE - 1)) // TILE) + 1
    n_row = -(-max_tiles * TILE // (16 * LANES)) * 16
    return pl.pallas_call(
        moe_kernel,
        out_shape=jax.ShapeDtypeStruct((n_tok, chunks, LANES), jnp.bfloat16),
        in_specs=[pl.BlockSpec(memory_space=pltpu.VMEM)] + [hbm] * 6,
        out_specs=hbm,
        scratch_shapes=[
            pltpu.VMEM((n_tok + GROUP, chunks, LANES), jnp.bfloat16),
            pltpu.VMEM((n_tok + GROUP, chunks, LANES), jnp.float32),
            pltpu.VMEM((2, width, hidden), jnp.bfloat16),
            pltpu.VMEM((2, width, hidden), jnp.bfloat16),
            pltpu.VMEM((2, width, hidden), jnp.bfloat16),
            pltpu.VMEM((chunks * PITCH + 8, LANES), jnp.float32),
            pltpu.VMEM((TILE, hidden), jnp.bfloat16),
            pltpu.VMEM((TILE, width), jnp.bfloat16),
            pltpu.VMEM((chunks * PITCH + 8, LANES), jnp.float32),
            pltpu.VMEM(idx.shape, jnp.int32),
            pltpu.VMEM((n_row + 16, LANES), jnp.int32),
            pltpu.SMEM((n_row + 16, LANES), jnp.int32),
            pltpu.SMEM((max_tiles + 1,), jnp.int32),
            pltpu.SMEM(wt.shape, jnp.float32),
            pltpu.SemaphoreType.DMA,
            pltpu.SemaphoreType.DMA,
            pltpu.SemaphoreType.DMA((2, 3)),
            pltpu.SemaphoreType.DMA,
            pltpu.SemaphoreType.DMA,
            pltpu.SemaphoreType.DMA,
        ],
        compiler_params=pltpu.CompilerParams(vmem_limit_bytes=67043328),
        cost_estimate=pl.CostEstimate(flops=2 * 3 * hidden * width * n_tok, bytes_accessed=130_000_000, transcendentals=0),
        name="moe",
    )(idx, wt, h3, sums, eg, eu, ed)


def front_kernel(hid, gain_ref, head_ref, sig_ref, own_idx, sg, su, sd, h_out, sum_out, wt_out, idx_out,
                 idx_ref, wg, wu, wd, hbuf, x4, xb, act, y4, stage, t4, h_sem, s_sem, pair_send, pair_recv, y_send, y_recv, z_send, z_recv,
                 fwd_send, fwd_recv, w_sem, i_send, i_recv):
    z, e = lax.axis_index("tp"), lax.axis_index("ep")
    rows, hidden = hid.shape
    chunks = hidden // LANES
    size = t4.shape[0] // chunks - 1
    n_chunk = rows // (2 * size)
    core = e % 2
    pair = e + 1 - 2 * core
    far = (e + 2) % 4
    far_pair = (pair + 2) % 4
    half = z % 2
    zpair = z + 1 - 2 * half

    barrier = pltpu.get_barrier_semaphore()
    for dev in ({"ep": pair}, {"ep": far}, {"ep": far_pair}, {"tp": zpair}):
        pl.semaphore_signal(barrier, inc=1, device_id=dev, device_id_type=MESH)
    w_copies = [pltpu.make_async_copy(s, d, w_sem.at[i])
                for i, (s, d) in enumerate(((sg, wg), (su, wu), (sd, wd)))]
    for c in w_copies:
        c.start()
    pl.semaphore_wait(barrier, 4)

    i_copies = [pltpu.make_async_remote_copy(
        own_idx, idx_ref.at[e], i_send.at[i], i_recv.at[i], device_id={"ep": dev}, device_id_type=MESH)
        for i, dev in enumerate((pair, far, far_pair))]
    for c in i_copies:
        c.start()
    idx_ref[e] = own_idx[...]

    def send_rows(block, h, j):
        return hbuf.at[pl.ds(block * rows + h * (rows // 2) + j * size, size)]

    def y_copy(j):
        mine = send_rows(e, half, j)
        return pltpu.make_async_remote_copy(mine, mine, y_send.at[j], y_recv.at[j], device_id={"ep": far}, device_id_type=MESH)

    def z_copy(j):
        got = send_rows(far, half, j)
        return pltpu.make_async_remote_copy(got, got, z_send.at[j], z_recv.at[j], device_id={"tp": zpair}, device_id_type=MESH)

    def fwd_copy(j, side):
        got = send_rows(far, half if side == 0 else 1 - half, j)
        return pltpu.make_async_remote_copy(
            got, got, fwd_send.at[side, j], fwd_recv.at[side, j], device_id={"ep": pair}, device_id_type=MESH)

    own = hbuf.at[pl.ds(e * rows, rows)]
    to_pair = pltpu.make_async_remote_copy(own, own, pair_send, pair_recv, device_id={"ep": pair}, device_id_type=MESH)
    gain = gain_ref[...].astype(jnp.float32)

    def norm(c, _):
        lo = (half * n_chunk + c) % (2 * n_chunk) * size
        x = hid[pl.ds(lo, size), :].astype(jnp.float32)
        inv_rms = lax.rsqrt(jnp.mean(x * x, axis=-1, keepdims=True) + RMS_EPS)
        h = (x * inv_rms * gain).astype(jnp.bfloat16).astype(jnp.float32)
        for k in range(chunks):
            t4[k * (size + 1):k * (size + 1) + size, :] = h[:, k * LANES:(k + 1) * LANES]
        for i in range(size):
            hbuf[e * rows + lo + i] = t4[pl.ds(i, chunks, stride=size + 1), :].astype(jnp.bfloat16)

        @pl.when(c < n_chunk)
        def _():
            y_copy(c).start()
        return 0
    lax.fori_loop(0, 2 * n_chunk, norm, 0)
    to_pair.start()
    for c in w_copies:
        c.wait()

    def relay_y(j):
        y_copy(j).wait_recv()
        z_copy(j).start()
        fwd_copy(j, 0).start()

    def relay_z(j):
        z_copy(j).wait_recv()
        fwd_copy(j, 1).start()

    n_tile = 4 * rows // TILE
    per = rows // TILE
    quarter = n_chunk // 2
    half_step, flight = 1.7, 45.0 / n_chunk
    due = {}
    for j in range(n_chunk):
        y_at = 5 + flight * (j + 1)
        for kind, at_time, need in (("y", y_at, 16 if j < quarter else 24), ("z", y_at + flight + 3, 20 if j < quarter else 28)):
            q = min(need, max(0, math.ceil((at_time - 5) / half_step)))
            due.setdefault(q, []).append((at_time, kind, j))
    due.setdefault(8, []).append((0, "p", 0))
    for q, kind, j in ((18, "a", 0), (22, "b", 0), (26, "a", 1), (30, "b", 1)):
        due.setdefault(q, []).append((1e3, kind, j))

    def h_rows(base):
        return pltpu.make_async_copy(hbuf.at[pl.ds(base, TILE)], h_out.at[pl.ds(base, TILE)], h_sem)

    def do(what):
        _, kind, arg = what
        if kind == "p":
            to_pair.wait_recv()
            for c in i_copies:
                c.wait_recv()
            ranks, n_top, _ = idx_ref.shape
            nb = rows // LANES
            for r in range(ranks * n_top * nb):
                b = r % nb
                idx_out[r:r + 1, :] = idx_ref[r // (n_top * nb), r // nb % n_top:r // nb % n_top + 1, b * LANES:(b + 1) * LANES]
        elif kind == "y":
            relay_y(arg)
        elif kind == "z":
            relay_z(arg)
        else:
            for j in range(quarter):
                fwd_copy(arg * quarter + j, 0 if kind == "a" else 1).wait_recv()

    def sum_copy(base, slot):
        return pltpu.make_async_copy(stage.at[slot], sum_out.at[pl.ds(base, TILE)], s_sem.at[slot])

    sig = sig_ref[...].astype(jnp.float32)

    def relay(q, parity):
        for at_step, what in due.items():
            if at_step % 2 == parity:
                @pl.when(q == at_step)
                def _(what=what):
                    for w in sorted(what):
                        do(w)

    def tile(s, _):
        relay(2 * s, 0)
        u = s - 2 * per
        near = s // per
        near_block = e + near * (pair - e)
        near_base = near_block * rows + s % per * TILE
        far_block = far + u % 2 * (far_pair - far)
        far_half = half + u // 2 % 2 * (1 - 2 * half)
        far_base = far_block * rows + far_half * (rows // 2) + u // 4 * TILE
        is_far = s // (2 * per)
        base = pl.multiple_of(near_base + is_far * (far_base - near_base), TILE)
        block = near_block + is_far * (far_block - near_block)
        col = pl.multiple_of(base - block * rows, TILE)
        slot = s % 2

        def fill(g, _):
            for v in range(16):
                i = g * 16 + v
                x4[pl.ds(i, chunks, stride=PITCH), :] = hbuf[base + i].astype(jnp.float32)
            return 0
        lax.fori_loop(0, TILE // 16, fill, 0)
        for k in range(chunks):
            xb[:, k * LANES:(k + 1) * LANES] = x4[k * PITCH:k * PITCH + TILE, :].astype(jnp.bfloat16)

        logits = dot_t(head_ref[...], xb[...])
        prob = jnp.exp(logits - jnp.max(logits, axis=0, keepdims=True))
        prob = prob / jnp.sum(prob, axis=0, keepdims=True)
        expert = lax.broadcasted_iota(jnp.int32, prob.shape, 0)
        idx = idx_ref[block, :, pl.ds(col, TILE)]
        picked = [jnp.sum(jnp.where(expert == idx[k:k + 1, :], prob, 0.0), axis=0, keepdims=True) for k in range(idx.shape[0])]
        wt_out[:, pl.ds(base, TILE)] = jnp.concatenate(picked, axis=0)

        gate = dot_t(xb[...], wg[...])
        up = dot_t(xb[...], wu[...])
        act[...] = (jax.nn.silu(gate) * up).astype(jnp.bfloat16)
        scale = jax.nn.sigmoid(jnp.sum(xb[...].astype(jnp.float32) * sig, axis=1, keepdims=True))
        for k in range(0, chunks, 2):
            d = jnp.dot(act[...], wd[:, k * LANES:(k + 2) * LANES], preferred_element_type=jnp.float32) * scale
            y4[k * PITCH:k * PITCH + TILE, :] = d[:, :LANES]
            y4[(k + 1) * PITCH:(k + 1) * PITCH + TILE, :] = d[:, LANES:]

        relay(2 * s + 1, 1)
        h_rows(base).start()

        @pl.when(s >= 2)
        def _():
            sum_copy(0, slot).wait()

        def put(g, _):
            for v in range(16):
                i = g * 16 + v
                stage[slot, i] = y4[pl.ds(i, chunks, stride=PITCH), :]
            return 0
        lax.fori_loop(0, TILE // 16, put, 0)
        sum_copy(base, slot).start()
        return 0
    lax.fori_loop(0, n_tile, tile, 0)

    def drain(j, _):
        fwd_copy(j, 0).wait_send()
        fwd_copy(j, 1).wait_send()
        y_copy(j).wait_send()
        z_copy(j).wait_send()
        return 0
    lax.fori_loop(0, n_chunk, drain, 0)
    to_pair.wait_send()
    for c in i_copies:
        c.wait_send()
    pltpu.make_async_copy(hbuf, h_out, h_sem).wait()
    sum_copy(0, 0).wait()
    sum_copy(0, 1).wait()


def front(hidden_in, gain, head, sig, own_idx, ranks, sg, su, sd):
    rows, hidden = hidden_in.shape
    n_top = own_idx.shape[0]
    width = sg.shape[0]
    chunks = hidden // LANES
    n_tok = ranks * rows
    size = rows // (2 * SPREAD_CHUNKS)
    dma = pltpu.SemaphoreType.DMA
    vmem = pl.BlockSpec(memory_space=pltpu.VMEM)
    hbm = pl.BlockSpec(memory_space=pl.ANY)
    pitched = pltpu.VMEM((chunks * PITCH + 8, LANES), jnp.float32)
    return pl.pallas_call(
        front_kernel,
        out_shape=(jax.ShapeDtypeStruct((n_tok, chunks, LANES), jnp.bfloat16),
                   jax.ShapeDtypeStruct((n_tok, chunks, LANES), jnp.float32),
                   jax.ShapeDtypeStruct((n_top, TOK_MASK + 1), jnp.float32),
                   jax.ShapeDtypeStruct((n_tok * n_top // LANES, LANES), jnp.int32)),
        in_specs=[vmem] * 5 + [hbm] * 3,
        out_specs=(hbm, hbm, vmem, vmem),
        scratch_shapes=[
            pltpu.VMEM((ranks, n_top, rows), jnp.int32), pltpu.VMEM((width, hidden), jnp.bfloat16),
            pltpu.VMEM((width, hidden), jnp.bfloat16), pltpu.VMEM((width, hidden), jnp.bfloat16),
            pltpu.VMEM((n_tok, chunks, LANES), jnp.bfloat16), pitched, pltpu.VMEM((TILE, hidden), jnp.bfloat16),
            pltpu.VMEM((TILE, width), jnp.bfloat16), pitched, pltpu.VMEM((2, TILE, chunks, LANES), jnp.float32),
            pltpu.VMEM((chunks * (size + 1), LANES), jnp.float32),
            dma, dma((2,)), dma, dma] + [dma((SPREAD_CHUNKS,))] * 4 + [dma((2, SPREAD_CHUNKS))] * 2
        + [dma((3,)), dma((3,)), dma((3,))],
        compiler_params=pltpu.CompilerParams(collective_id=0, has_side_effects=True, vmem_limit_bytes=60 << 20),
        name="front",
    )(hidden_in, gain, head, sig, own_idx, sg, su, sd)


def combine_kernel(n_chunk, lag, part, hid_hbm, out_ref, mine, near, far_in, zin, hid, t4, m_sem, h_sem,
                   d_send, d_recv, y_send, y_recv, z_send, z_recv, t_send):
    z, e = lax.axis_index("tp"), lax.axis_index("ep")
    rows = out_ref.shape[0]
    chunks = part.shape[1]
    size = rows // n_chunk
    core = e % 2
    pair = e + 1 - 2 * core
    far = (e + 2) % 4
    far_pair = (pair + 2) % 4
    n_z = 4
    zn = z + 1 - 2 * (z % 2)

    barrier = pltpu.get_barrier_semaphore()
    for dev in ({"ep": pair}, {"ep": far}):
        pl.semaphore_signal(barrier, inc=1, device_id=dev, device_id_type=MESH)

    @pl.when(z > 0)
    def _():
        pl.semaphore_signal(barrier, inc=1, device_id={"tp": z - 1}, device_id_type=MESH)

    @pl.when(z < n_z - 1)
    def _():
        pl.semaphore_signal(barrier, inc=1, device_id={"tp": z + 1}, device_id_type=MESH)
    at_end = (z == 0) | (z == n_z - 1)

    @pl.when(at_end)
    def _():
        pl.semaphore_wait(barrier, 3)

    @pl.when(jnp.logical_not(at_end))
    def _():
        pl.semaphore_wait(barrier, 4)

    def at(j):
        return pl.ds(j * size, size)

    def d_copy(j, side):
        owner = far_pair if side == 0 else pair
        return pltpu.make_async_remote_copy(
            part.at[pl.ds(owner * rows + j * size, size)], near.at[side, at(j)],
            d_send.at[side, j], d_recv.at[side, j], device_id={"ep": pair}, device_id_type=MESH)

    def m_copy(j, side):
        owner = far if side == 0 else e
        return pltpu.make_async_copy(part.at[pl.ds(owner * rows + j * size, size)], mine.at[side, at(j)], m_sem.at[side, j])

    def y_copy(j):
        return pltpu.make_async_remote_copy(
            mine.at[0, at(j)], far_in.at[at(j)], y_send.at[j], y_recv.at[j], device_id={"ep": far}, device_id_type=MESH)

    def z_copy(j, slot, to):
        return pltpu.make_async_remote_copy(
            mine.at[1, at(j)], zin.at[slot, at(j)], z_send.at[j], z_recv.at[slot, j], device_id={"tp": to}, device_id_type=MESH)

    def t_copy(j, side, to, src):
        return pltpu.make_async_remote_copy(
            src, zin.at[1, at(j)], t_send.at[side, j], z_recv.at[1, j], device_id={"tp": to}, device_id_type=MESH)

    hid_copy = pltpu.make_async_copy(hid_hbm, hid, h_sem)

    def first(j, _):
        for side in range(2):
            d_copy(j, side).start()
            m_copy(j, side).start()
        return 0
    lax.fori_loop(0, n_chunk, first, 0)
    hid_copy.start()

    def f32(ref):
        return ref[...].astype(jnp.float32)

    def finish(j, src):
        def put(g, _):
            for u in range(8):
                i = g * 8 + u
                t4[pl.ds(i, chunks, stride=size + 1), :] = src[i].astype(jnp.float32)
            return 0
        lax.fori_loop(0, size // 8, put, 0)
        for k in range(chunks):
            cols = slice(k * LANES, (k + 1) * LANES)
            tot = t4[k * (size + 1):k * (size + 1) + size, :]
            out_ref[at(j), cols] = (hid[at(j), cols].astype(jnp.float32) + tot).astype(jnp.bfloat16)

    def step(i, _):
        @pl.when(i < n_chunk)
        def _():
            for side in range(2):
                d_copy(i, side).wait_recv()
                m_copy(i, side).wait()
            mine[0, at(i)] = (f32(mine.at[0, at(i)]) + f32(near.at[0, at(i)])).astype(jnp.bfloat16)
            y_copy(i).start()

        def stage(shift):
            j = i - shift * lag
            odd = j % 2
            spot = z + odd * (n_z - 1 - 2 * z)
            ahead = 1 - 2 * odd
            return j, spot, ahead, (j >= 0) & (j < n_chunk)

        @pl.when(i == 3 * lag)
        def _():
            hid_copy.wait()

        j, spot, ahead, live = stage(1)

        @pl.when(live)
        def _():
            y_copy(j).wait_recv()
            mine[1, at(j)] = (f32(mine.at[1, at(j)]) + f32(near.at[1, at(j)]) + f32(far_in.at[at(j)])).astype(jnp.bfloat16)

            @pl.when(spot == 0)
            def _():
                z_copy(j, 0, z + ahead).start()

            @pl.when(spot == 3)
            def _():
                z_copy(j, 0, z - ahead).start()

        j2, spot2, ahead2, live2 = stage(2)

        @pl.when(live2 & (spot2 == 2))
        def _():
            z_copy(j2, 0, zn).wait_recv()
            mine[1, at(j2)] = (f32(mine.at[1, at(j2)]) + f32(zin.at[0, at(j2)])).astype(jnp.bfloat16)
            z_copy(j2, 1, z - ahead2).start()

        j3, spot3, ahead3, live3 = stage(3)

        @pl.when(live3 & (spot3 == 1))
        def _():
            z_copy(j3, 0, zn).wait_recv()
            z_copy(j3, 1, zn).wait_recv()
            mine[1, at(j3)] = (f32(mine.at[1, at(j3)]) + f32(zin.at[0, at(j3)]) + f32(zin.at[1, at(j3)])).astype(jnp.bfloat16)
            t_copy(j3, 0, z - ahead3, mine.at[1, at(j3)]).start()
            t_copy(j3, 1, z + ahead3, mine.at[1, at(j3)]).start()
            finish(j3, mine.at[1, at(j3)])

        j4, spot4, ahead4, live4 = stage(4)

        @pl.when(live4 & (spot4 == 2))
        def _():
            z_copy(j4, 1, zn).wait_recv()
            t_copy(j4, 0, z + ahead4, zin.at[1, at(j4)]).start()
            finish(j4, zin.at[1, at(j4)])

        j5, spot5, ahead5, live5 = stage(5)

        @pl.when(live5 & ((spot5 == 0) | (spot5 == 3)))
        def _():
            z_copy(j5, 1, zn).wait_recv()
            finish(j5, zin.at[1, at(j5)])
        return 0
    lax.fori_loop(0, n_chunk + 5 * lag, step, 0)

    def drain(j, _):
        odd = j % 2
        spot = z + odd * (n_z - 1 - 2 * z)
        d_copy(j, 0).wait_send()
        d_copy(j, 1).wait_send()
        y_copy(j).wait_send()

        @pl.when(spot != 1)
        def _():
            z_copy(j, 0, zn).wait_send()

        @pl.when((spot == 1) | (spot == 2))
        def _():
            t_copy(j, 0, zn, mine.at[1, at(j)]).wait_send()

        @pl.when(spot == 1)
        def _():
            t_copy(j, 1, zn, mine.at[1, at(j)]).wait_send()
        return 0
    lax.fori_loop(0, n_chunk, drain, 0)


def combine(part, hidden_in, n_chunk, lag):
    rows, hidden = hidden_in.shape
    block = (rows,) + part.shape[1:]
    dma = pltpu.SemaphoreType.DMA
    size = rows // n_chunk
    hbm = pl.BlockSpec(memory_space=pl.ANY)
    return pl.pallas_call(
        functools.partial(combine_kernel, n_chunk, lag),
        out_shape=jax.ShapeDtypeStruct((rows, hidden), jnp.bfloat16),
        in_specs=[hbm, hbm],
        out_specs=pl.BlockSpec(memory_space=pltpu.VMEM),
        scratch_shapes=[
            pltpu.VMEM((2,) + block, jnp.bfloat16), pltpu.VMEM((2,) + block, jnp.bfloat16), pltpu.VMEM(block, jnp.bfloat16),
            pltpu.VMEM((2,) + block, jnp.bfloat16), pltpu.VMEM((rows, hidden), jnp.bfloat16),
            pltpu.VMEM(((size + 1) * part.shape[1] + 8, LANES), jnp.float32),
            dma((2, n_chunk)), dma, dma((2, n_chunk)), dma((2, n_chunk)), dma((n_chunk,)), dma((n_chunk,)),
            dma((n_chunk,)), dma((2, n_chunk)), dma((2, n_chunk)),
        ],
        compiler_params=pltpu.CompilerParams(collective_id=1, has_side_effects=True, vmem_limit_bytes=60 << 20),
        name="combine",
    )(part, hidden_in)


def solution(mesh):
    tok_spec = P(('dp', 'ep'), None)
    in_specs = (tok_spec, tok_spec, P(None), P(None, None), P(None, None),
                P('ep', None, 'tp'), P('ep', None, 'tp'), P('ep', 'tp', None),
                P(None, ('tp', 'ep')), P(None, ('tp', 'ep')), P(('tp', 'ep'), None))

    def local_step(hidden_in, topk_idx, norm_gain, router_w, shared_sig_w, exp_gate, exp_up, exp_down, sh_gate, sh_up, sh_down):
        all_h, sums, wt, all_idx = front(hidden_in, norm_gain[None, :], router_w.T, shared_sig_w.T, topk_idx.T,
                                         lax.axis_size('ep'), sh_gate.T, sh_up.T, sh_down)
        part = moe(all_idx, wt.reshape(-1), all_h, sums, jnp.swapaxes(exp_gate, 1, 2), jnp.swapaxes(exp_up, 1, 2), exp_down)
        return combine(part, hidden_in, COMBINE_CHUNKS, COMBINE_LAG)

    return jax.shard_map(local_step, mesh=mesh, in_specs=in_specs, out_specs=tok_spec, check_vma=False)
```

profile of v0, /device:TPU:0, one launch (start us, length us, event | category | flops | bytes accessed | tf_op | source)
XLA Modules:
  0.0 293.3 jit_solution(15556005933675536125)
XLA Ops:
  0.0 1.3 broadcast_in_dim.3.gain_ref
  1.3 75.8 %front.1 = (bf16[4096,16,128]{2,1,0:T(8,128)(2,1)}, f32[4096,16,128]{2,1,0:T(8,128)}, f32[4,8192]{1,0:T(4,128)}, s32[128,128]{1,0:T(8,128)}) custom-call(bf16[1024,2048]{1,0:T(8,128)(2,1)} %hid_hbm.1, bf16[1,2048]{1,0:T(2,128)(2,1)} %broadcast_in_dim.3.gain_ref, bf16[60,2048]{1,0:T(8,128)(2,1)} %bitcast.14, bf16[1,2048]{1,0:T(2,128)(2,1)} %bitcast.17, ...), custom_call_target="tpu_custom_call" | custom-call | tf_op jit(solution)/shard_map/front/pallas_call | solution.py:456
  77.1 1.6 copy.12
  78.7 90.0 %moe.1.part = bf16[4096,16,128]{2,1,0:T(8,128)(2,1)} custom-call(s32[128,128]{1,0:T(8,128)} %get-tuple-element.9.idx_ref, f32[32768]{0:T(1024)} %bitcast.13, bf16[4096,16,128]{2,1,0:T(8,128)(2,1)} %get-tuple-element.11.h_hbm, f32[4096,16,128]{2,1,0:T(8,128)} %get-tuple-element.12.sum_hbm, bf16[15,352,2048]{2,1,0:T(8,128)(2,1)} %bitcast.9, ...), custom_call_target="tpu_custom_call" | custom-call | flops 17716740096 | bytes 130000000 | tf_op jit(solution)/shard_map/moe/pallas_call | solution.py:211
  168.7 119.8 %combine.1 = bf16[1024,2048]{1,0:T(8,128)(2,1)} custom-call(bf16[4096,16,128]{2,1,0:T(8,128)(2,1)} %moe.1.part, bf16[1024,2048]{1,0:T(8,128)(2,1)} %hid_hbm.1), custom_call_target="tpu_custom_call" | custom-call | tf_op jit(solution)/shard_map/combine/pallas_call | solution.py:660
  288.6 4.8 %copy.14 = bf16[1024,2048]{1,0:T(8,128)(2,1)} copy(bf16[1024,2048]{1,0:T(8,128)(2,1)} %combine.1) | data formatting | bytes 8388608
where the time goes:
time: 295 us; the launch traced here: 293 us
  Pallas kernels  286 us (97%)
  local copies, waits for them, and re-layouts  7.65 us (3%)
    pallas_call x1, Pallas kernels, combine(): pl.pallas_call(functools.partial(combine_kernel, n_chunk, lag), out_shape...  120 us
    pallas_call x1, Pallas kernels, moe(): pl.pallas_call(moe_kernel, out_shape=jax.ShapeDtypeStruct((n_tok, chunks,...  90 us
    pallas_call x1, Pallas kernels, front(): pl.pallas_call(front_kernel, out_shape=(jax.ShapeDtypeStruct((n_tok, chun...  75.8 us
    unnamed x2, local copies, waits for them, and re-layouts  6.36 us

commit v1 on v0

--- a/solution.py
+++ b/solution.py
@@ -83,9 +83,20 @@
     span = TILE // LANES
     last = n_row // span - 1
 
-    def weight_copies(e, slot):
-        return [pltpu.make_async_copy(s.at[e], d.at[slot], w_sem.at[slot, i])
-                for i, (s, d) in enumerate(((eg, wg), (eu, wu), (ed, wd)))]
+    def weight_starts(e, slot):
+        def start(k, _):
+            cols = pl.ds(pl.multiple_of(k * LANES, LANES), LANES)
+            for i, (s, d) in enumerate(((eg, wg), (eu, wu), (ed, wd))):
+                pltpu.make_async_copy(s.at[e, :, cols], d.at[slot, k], w_sem.at[slot, i]).start()
+            return 0
+        lax.fori_loop(0, chunks, start, 0)
+
+    def weight_waits(slot):
+        for i, d in enumerate((wg, wu, wd)):
+            pltpu.make_async_copy(d.at[slot], d.at[slot], w_sem.at[slot, i]).wait()
+
+    def columns(ref, lo, hi):
+        return jnp.concatenate([ref[k] for k in range(lo, hi)], axis=1)
 
     h_copy = pltpu.make_async_copy(h_hbm, hv.at[pl.ds(0, n_tok)], h_sem)
     s_copy = pltpu.make_async_copy(sum_hbm, acc.at[pl.ds(0, n_tok)], s_sem)
@@ -112,8 +123,7 @@
 
     @pl.when(n_tile > 0)
     def _():
-        for c in weight_copies(tile_exp[0], 0):
-            c.start()
+        weight_starts(tile_exp[0], 0)
     h_copy.wait()
     t_copy.wait()
 
@@ -124,7 +134,7 @@
             x4[pl.ds(i, chunks, stride=PITCH), :] = hv[tok].astype(jnp.float32)
 
     def pack(k):
-        xb[:, k * LANES:(k + 1) * LANES] = x4[k * PITCH:k * PITCH + TILE, :].astype(jnp.bfloat16)
+        xb[k] = x4[k * PITCH:k * PITCH + TILE, :].astype(jnp.bfloat16)
 
     def scatter(base, g):
         sums = []
@@ -150,14 +160,12 @@
 
         @pl.when(fresh)
         def _():
-            for c in weight_copies(e, slot):
-                c.wait()
+            weight_waits(slot)
             after = t + exp_tiles(e)
 
             @pl.when(after < n_tile)
             def _():
-                for c in weight_copies(tile_exp[after], 1 - slot):
-                    c.start()
+                weight_starts(tile_exp[after], 1 - slot)
 
         @pl.when(t == 1)
         def _():
@@ -165,15 +173,16 @@
 
         prev = jnp.where(t == 0, last, t - 1)
         n_group = TILE // GROUP
-        gate = dot_t(xb[...], wg[slot])
-        up = dot_t(xb[...], wu[slot])
+        x = columns(xb, 0, chunks)
+        gate = dot_t(x, columns(wg.at[slot], 0, chunks))
+        up = dot_t(x, columns(wu.at[slot], 0, chunks))
         for g in range(n_group):
             scatter(prev, g)
         act[...] = (jax.nn.silu(gate) * up).astype(jnp.bfloat16)
         for g in range(n_group):
             gather(t + 1, g)
         for k in range(0, chunks, 2):
-            d = jnp.dot(act[...], wd[slot, :, k * LANES:(k + 2) * LANES], preferred_element_type=jnp.float32)
+            d = jnp.dot(act[...], columns(wd.at[slot], k, k + 2), preferred_element_type=jnp.float32)
             y4[k * PITCH:k * PITCH + TILE, :] = d[:, :LANES]
             y4[(k + 1) * PITCH:(k + 1) * PITCH + TILE, :] = d[:, LANES:]
         for k in range(chunks):
@@ -216,11 +225,11 @@
         scratch_shapes=[
             pltpu.VMEM((n_tok + GROUP, chunks, LANES), jnp.bfloat16),
             pltpu.VMEM((n_tok + GROUP, chunks, LANES), jnp.float32),
-            pltpu.VMEM((2, width, hidden), jnp.bfloat16),
-            pltpu.VMEM((2, width, hidden), jnp.bfloat16),
-            pltpu.VMEM((2, width, hidden), jnp.bfloat16),
+            pltpu.VMEM((2, chunks, width, LANES), jnp.bfloat16),
+            pltpu.VMEM((2, chunks, width, LANES), jnp.bfloat16),
+            pltpu.VMEM((2, chunks, width, LANES), jnp.bfloat16),
             pltpu.VMEM((chunks * PITCH + 8, LANES), jnp.float32),
-            pltpu.VMEM((TILE, hidden), jnp.bfloat16),
+            pltpu.VMEM((chunks, TILE, LANES), jnp.bfloat16),
             pltpu.VMEM((TILE, width), jnp.bfloat16),
             pltpu.VMEM((chunks * PITCH + 8, LANES), jnp.float32),
             pltpu.VMEM(idx.shape, jnp.int32),
@@ -290,7 +299,7 @@
 
     own = hbuf.at[pl.ds(e * rows, rows)]
     to_pair = pltpu.make_async_remote_copy(own, own, pair_send, pair_recv, device_id={"ep": pair}, device_id_type=MESH)
-    gain = gain_ref[...].astype(jnp.float32)
+    gain = gain_ref[...].astype(jnp.float32).reshape(1, -1)
 
     def norm(c, _):
         lo = (half * n_chunk + c) % (2 * n_chunk) * size
@@ -474,7 +483,7 @@
     )(hidden_in, gain, head, sig, own_idx, sg, su, sd)
 
 
-def combine_kernel(n_chunk, lag, part, hid_hbm, out_ref, mine, near, far_in, zin, hid, t4, m_sem, h_sem,
+def combine_kernel(n_chunk, lag, part, hid, out_ref, mine, near, far_in, zin, t4, m_sem,
                    d_send, d_recv, y_send, y_recv, z_send, z_recv, t_send):
     z, e = lax.axis_index("tp"), lax.axis_index("ep")
     rows = out_ref.shape[0]
@@ -533,15 +542,12 @@
         return pltpu.make_async_remote_copy(
             src, zin.at[1, at(j)], t_send.at[side, j], z_recv.at[1, j], device_id={"tp": to}, device_id_type=MESH)
 
-    hid_copy = pltpu.make_async_copy(hid_hbm, hid, h_sem)
-
     def first(j, _):
         for side in range(2):
             d_copy(j, side).start()
             m_copy(j, side).start()
         return 0
     lax.fori_loop(0, n_chunk, first, 0)
-    hid_copy.start()
 
     def f32(ref):
         return ref[...].astype(jnp.float32)
@@ -574,10 +580,6 @@
             ahead = 1 - 2 * odd
             return j, spot, ahead, (j >= 0) & (j < n_chunk)
 
-        @pl.when(i == 3 * lag)
-        def _():
-            hid_copy.wait()
-
         j, spot, ahead, live = stage(1)
 
         @pl.when(live)
@@ -660,16 +662,16 @@
     return pl.pallas_call(
         functools.partial(combine_kernel, n_chunk, lag),
         out_shape=jax.ShapeDtypeStruct((rows, hidden), jnp.bfloat16),
-        in_specs=[hbm, hbm],
+        in_specs=[hbm, pl.BlockSpec(memory_space=pltpu.VMEM)],
         out_specs=pl.BlockSpec(memory_space=pltpu.VMEM),
         scratch_shapes=[
             pltpu.VMEM((2,) + block, jnp.bfloat16), pltpu.VMEM((2,) + block, jnp.bfloat16), pltpu.VMEM(block, jnp.bfloat16),
-            pltpu.VMEM((2,) + block, jnp.bfloat16), pltpu.VMEM((rows, hidden), jnp.bfloat16),
+            pltpu.VMEM((2,) + block, jnp.bfloat16),
             pltpu.VMEM(((size + 1) * part.shape[1] + 8, LANES), jnp.float32),
-            dma((2, n_chunk)), dma, dma((2, n_chunk)), dma((2, n_chunk)), dma((n_chunk,)), dma((n_chunk,)),
+            dma((2, n_chunk)), dma((2, n_chunk)), dma((2, n_chunk)), dma((n_chunk,)), dma((n_chunk,)),
             dma((n_chunk,)), dma((2, n_chunk)), dma((2, n_chunk)),
         ],
-        compiler_params=pltpu.CompilerParams(collective_id=1, has_side_effects=True, vmem_limit_bytes=60 << 20),
+        compiler_params=pltpu.CompilerParams(collective_id=1, has_side_effects=True, vmem_limit_bytes=40 << 20),
         name="combine",
     )(part, hidden_in)
 
@@ -681,7 +683,7 @@
                 P(None, ('tp', 'ep')), P(None, ('tp', 'ep')), P(('tp', 'ep'), None))
 
     def local_step(hidden_in, topk_idx, norm_gain, router_w, shared_sig_w, exp_gate, exp_up, exp_down, sh_gate, sh_up, sh_down):
-        all_h, sums, wt, all_idx = front(hidden_in, norm_gain[None, :], router_w.T, shared_sig_w.T, topk_idx.T,
+        all_h, sums, wt, all_idx = front(hidden_in, norm_gain, router_w.T, shared_sig_w.T, topk_idx.T,
                                          lax.axis_size('ep'), sh_gate.T, sh_up.T, sh_down)
         part = moe(all_idx, wt.reshape(-1), all_h, sums, jnp.swapaxes(exp_gate, 1, 2), jnp.swapaxes(exp_up, 1, 2), exp_down)
         return combine(part, hidden_in, COMBINE_CHUNKS, COMBINE_LAG)

time: 295 us -> 297 us (level)
  the two profiles are of different devices: /device:TPU:0 before, /device:TPU:2 now
where the time goes in v1:
time: 297 us
  Pallas kernels  291 us (98%)
  local copies, waits for them, and re-layouts  5.77 us (2%)
    pallas_call x1, Pallas kernels, combine(): pl.pallas_call(functools.partial(combine_kernel, n_chunk, lag), out_shape...  157 us
    pallas_call x1, Pallas kernels, front(): pl.pallas_call(front_kernel, out_shape=(jax.ShapeDtypeStruct((n_tok, chun...  74.3 us
    pallas_call x1, Pallas kernels, moe(): pl.pallas_call(moe_kernel, out_shape=jax.ShapeDtypeStruct((n_tok, chunks,...  59.7 us

profile of v1, /device:TPU:2, one launch (start us, length us, event | category | flops | bytes accessed | tf_op | source)
XLA Modules:
  0.0 297.2 jit_solution(5988920981176492781)
XLA Ops:
  0.0 74.3 %front.1 = (bf16[4096,16,128]{2,1,0:T(8,128)(2,1)}, f32[4096,16,128]{2,1,0:T(8,128)}, f32[4,8192]{1,0:T(4,128)}, s32[128,128]{1,0:T(8,128)}) custom-call(bf16[1024,2048]{1,0:T(8,128)(2,1)} %hid.3, bf16[2048]{0:T(1024)(128)(2,1)} %gain_ref.1, bf16[60,2048]{1,0:T(8,128)(2,1)} %bitcast.14, bf16[1,2048]{1,0:T(2,128)(2,1)} %bitcast.17, s32[4,1024]{1,0:T(4,128)} %bitcast.16, ...), custom_call_target="tpu_custom_call" | custom-call | tf_op jit(solution)/shard_map/front/pallas_call | solution.py:465
  74.3 1.6 copy.12
  75.9 59.7 %moe.1.part = bf16[4096,16,128]{2,1,0:T(8,128)(2,1)} custom-call(s32[128,128]{1,0:T(8,128)} %get-tuple-element.9.idx_ref, f32[32768]{0:T(1024)} %bitcast.13, bf16[4096,16,128]{2,1,0:T(8,128)(2,1)} %get-tuple-element.11.h_hbm, f32[4096,16,128]{2,1,0:T(8,128)} %get-tuple-element.12.sum_hbm, bf16[15,352,2048]{2,1,0:T(8,128)(2,1)} %bitcast.9, ...), custom_call_target="tpu_custom_call" | custom-call | flops 17716740096 | bytes 130000000 | tf_op jit(solution)/shard_map/moe/pallas_call | solution.py:220
  135.5 0.0 copy-start
  135.6 2.2 copy-done
  137.7 157.4 %combine.1 = bf16[1024,2048]{1,0:T(8,128)(2,1)S(1)} custom-call(bf16[4096,16,128]{2,1,0:T(8,128)(2,1)} %moe.1.part, bf16[1024,2048]{1,0:T(8,128)(2,1)S(1)} %copy-done), custom_call_target="tpu_custom_call" | custom-call | tf_op jit(solution)/shard_map/combine/pallas_call | solution.py:662
  295.1 2.0 copy.14
Async XLA Ops:
  135.5 2.2 copy-start

commit v2 on v1

--- a/solution.py
+++ b/solution.py
@@ -22,6 +22,10 @@
 
 def dot_t(a, b):
     return lax.dot_general(a, b, (((1,), (1,)), ((), ())), preferred_element_type=jnp.float32)
+
+
+def columns(ref, lo, hi):
+    return jnp.concatenate([ref[k] for k in range(lo, hi)], axis=1)
 
 
 def routing(idx_ref, first, ranks, n_tok, n_local, n_row, pos_v, list_v, in_row, totals):
@@ -95,8 +99,6 @@
         for i, d in enumerate((wg, wu, wd)):
             pltpu.make_async_copy(d.at[slot], d.at[slot], w_sem.at[slot, i]).wait()
 
-    def columns(ref, lo, hi):
-        return jnp.concatenate([ref[k] for k in range(lo, hi)], axis=1)
 
     h_copy = pltpu.make_async_copy(h_hbm, hv.at[pl.ds(0, n_tok)], h_sem)
     s_copy = pltpu.make_async_copy(sum_hbm, acc.at[pl.ds(0, n_tok)], s_sem)
@@ -268,10 +270,13 @@
     barrier = pltpu.get_barrier_semaphore()
     for dev in ({"ep": pair}, {"ep": far}, {"ep": far_pair}, {"tp": zpair}):
         pl.semaphore_signal(barrier, inc=1, device_id=dev, device_id_type=MESH)
-    w_copies = [pltpu.make_async_copy(s, d, w_sem.at[i])
-                for i, (s, d) in enumerate(((sg, wg), (su, wu), (sd, wd)))]
-    for c in w_copies:
-        c.start()
+
+    def load_weights(k, _):
+        cols = pl.ds(pl.multiple_of(k * LANES, LANES), LANES)
+        for i, (s, d) in enumerate(((sg, wg), (su, wu), (sd, wd))):
+            pltpu.make_async_copy(s.at[:, cols], d.at[k], w_sem.at[i]).start()
+        return 0
+    lax.fori_loop(0, chunks, load_weights, 0)
     pl.semaphore_wait(barrier, 4)
 
     i_copies = [pltpu.make_async_remote_copy(
@@ -317,8 +322,8 @@
         return 0
     lax.fori_loop(0, 2 * n_chunk, norm, 0)
     to_pair.start()
-    for c in w_copies:
-        c.wait()
+    for i, d in enumerate((wg, wu, wd)):
+        pltpu.make_async_copy(d, d, w_sem.at[i]).wait()
 
     def relay_y(j):
         y_copy(j).wait_recv()
@@ -332,7 +337,7 @@
     n_tile = 4 * rows // TILE
     per = rows // TILE
     quarter = n_chunk // 2
-    half_step, flight = 1.7, 45.0 / n_chunk
+    half_step, flight = 1.9, 45.0 / n_chunk
     due = {}
     for j in range(n_chunk):
         y_at = 5 + flight * (j + 1)
@@ -400,22 +405,25 @@
             return 0
         lax.fori_loop(0, TILE // 16, fill, 0)
         for k in range(chunks):
-            xb[:, k * LANES:(k + 1) * LANES] = x4[k * PITCH:k * PITCH + TILE, :].astype(jnp.bfloat16)
-
-        logits = dot_t(head_ref[...], xb[...])
+            xb[k] = x4[k * PITCH:k * PITCH + TILE, :].astype(jnp.bfloat16)
+
+        x = columns(xb, 0, chunks)
+        logits = dot_t(head_ref[...], x)
         prob = jnp.exp(logits - jnp.max(logits, axis=0, keepdims=True))
         prob = prob / jnp.sum(prob, axis=0, keepdims=True)
         expert = lax.broadcasted_iota(jnp.int32, prob.shape, 0)
         idx = idx_ref[block, :, pl.ds(col, TILE)]
         picked = [jnp.sum(jnp.where(expert == idx[k:k + 1, :], prob, 0.0), axis=0, keepdims=True) for k in range(idx.shape[0])]
-        wt_out[:, pl.ds(base, TILE)] = jnp.concatenate(picked, axis=0)
-
-        gate = dot_t(xb[...], wg[...])
-        up = dot_t(xb[...], wu[...])
+        for k, row in enumerate(picked):
+            for b in range(TILE // LANES):
+                wt_out[pl.ds(k * ((TOK_MASK + 1) // LANES) + base // LANES + b, 1), :] = row[:, b * LANES:(b + 1) * LANES]
+
+        gate = dot_t(x, columns(wg, 0, chunks))
+        up = dot_t(x, columns(wu, 0, chunks))
         act[...] = (jax.nn.silu(gate) * up).astype(jnp.bfloat16)
-        scale = jax.nn.sigmoid(jnp.sum(xb[...].astype(jnp.float32) * sig, axis=1, keepdims=True))
+        scale = jax.nn.sigmoid(jnp.sum(x.astype(jnp.float32) * sig, axis=1, keepdims=True))
         for k in range(0, chunks, 2):
-            d = jnp.dot(act[...], wd[:, k * LANES:(k + 2) * LANES], preferred_element_type=jnp.float32) * scale
+            d = jnp.dot(act[...], columns(wd, k, k + 2), preferred_element_type=jnp.float32) * scale
             y4[k * PITCH:k * PITCH + TILE, :] = d[:, :LANES]
             y4[(k + 1) * PITCH:(k + 1) * PITCH + TILE, :] = d[:, LANES:]
 
@@ -466,14 +474,14 @@
         front_kernel,
         out_shape=(jax.ShapeDtypeStruct((n_tok, chunks, LANES), jnp.bfloat16),
                    jax.ShapeDtypeStruct((n_tok, chunks, LANES), jnp.float32),
-                   jax.ShapeDtypeStruct((n_top, TOK_MASK + 1), jnp.float32),
+                   jax.ShapeDtypeStruct((n_top * (TOK_MASK + 1) // LANES, LANES), jnp.float32),
                    jax.ShapeDtypeStruct((n_tok * n_top // LANES, LANES), jnp.int32)),
         in_specs=[vmem] * 5 + [hbm] * 3,
         out_specs=(hbm, hbm, vmem, vmem),
         scratch_shapes=[
-            pltpu.VMEM((ranks, n_top, rows), jnp.int32), pltpu.VMEM((width, hidden), jnp.bfloat16),
-            pltpu.VMEM((width, hidden), jnp.bfloat16), pltpu.VMEM((width, hidden), jnp.bfloat16),
-            pltpu.VMEM((n_tok, chunks, LANES), jnp.bfloat16), pitched, pltpu.VMEM((TILE, hidden), jnp.bfloat16),
+            pltpu.VMEM((ranks, n_top, rows), jnp.int32), pltpu.VMEM((chunks, width, LANES), jnp.bfloat16),
+            pltpu.VMEM((chunks, width, LANES), jnp.bfloat16), pltpu.VMEM((chunks, width, LANES), jnp.bfloat16),
+            pltpu.VMEM((n_tok, chunks, LANES), jnp.bfloat16), pitched, pltpu.VMEM((chunks, TILE, LANES), jnp.bfloat16),
             pltpu.VMEM((TILE, width), jnp.bfloat16), pitched, pltpu.VMEM((2, TILE, chunks, LANES), jnp.float32),
             pltpu.VMEM((chunks * (size + 1), LANES), jnp.float32),
             dma, dma((2,)), dma, dma] + [dma((SPREAD_CHUNKS,))] * 4 + [dma((2, SPREAD_CHUNKS))] * 2

time: 297 us -> 292 us (0.983)
  the two profiles are of different devices: /device:TPU:2 before, /device:TPU:0 now
where the time goes in v2:
time: 292 us; the launch traced here: 291 us
  Pallas kernels  287 us (98%)
  local copies, waits for them, and re-layouts  4.2 us (1%)
    pallas_call x1, Pallas kernels, combine(): pl.pallas_call(functools.partial(combine_kernel, n_chunk, lag), out_shape...  118 us
    pallas_call x1, Pallas kernels, moe(): pl.pallas_call(moe_kernel, out_shape=jax.ShapeDtypeStruct((n_tok, chunks,...  93.7 us
    pallas_call x1, Pallas kernels, front(): pl.pallas_call(front_kernel, out_shape=(jax.ShapeDtypeStruct((n_tok, chun...  75.5 us

profile of v2, /device:TPU:0, one launch (start us, length us, event | category | flops | bytes accessed | tf_op | source)
XLA Modules:
  0.0 291.2 jit_solution(15301688909847876311)
XLA Ops:
  0.0 75.5 %front.1 = (bf16[4096,16,128]{2,1,0:T(8,128)(2,1)}, f32[4096,16,128]{2,1,0:T(8,128)}, f32[256,128]{1,0:T(8,128)}, s32[128,128]{1,0:T(8,128)}) custom-call(bf16[1024,2048]{1,0:T(8,128)(2,1)} %hid.3, bf16[2048]{0:T(1024)(128)(2,1)} %gain_ref.1, bf16[60,2048]{1,0:T(8,128)(2,1)} %bitcast.12, bf16[1,2048]{1,0:T(2,128)(2,1)} %bitcast.15, s32[4,1024]{1,0:T(4,128)} %bitcast.14, ...), custom_call_target="tpu_custom_call" | custom-call | tf_op jit(solution)/shard_map/front/pallas_call | solution.py:473
  75.5 93.7 %moe.1.part = bf16[4096,16,128]{2,1,0:T(8,128)(2,1)} custom-call(s32[128,128]{1,0:T(8,128)} %get-tuple-element.9.idx_ref, f32[32768]{0:T(1024)} %bitcast.13, bf16[4096,16,128]{2,1,0:T(8,128)(2,1)} %get-tuple-element.11.h_hbm, f32[4096,16,128]{2,1,0:T(8,128)} %get-tuple-element.12.sum_hbm, bf16[15,352,2048]{2,1,0:T(8,128)(2,1)} %bitcast.8, ...), custom_call_target="tpu_custom_call" | custom-call | flops 17716740096 | bytes 130000000 | tf_op jit(solution)/shard_map/moe/pallas_call | solution.py:222
  169.3 0.0 copy-start
  169.3 2.2 copy-done
  171.5 117.7 %combine.1 = bf16[1024,2048]{1,0:T(8,128)(2,1)S(1)} custom-call(bf16[4096,16,128]{2,1,0:T(8,128)(2,1)} %moe.1.part, bf16[1024,2048]{1,0:T(8,128)(2,1)S(1)} %copy-done), custom_call_target="tpu_custom_call" | custom-call | tf_op jit(solution)/shard_map/combine/pallas_call | solution.py:670
  289.2 2.0 copy.13
Async XLA Ops:
  169.3 2.2 copy-start
